TPU v7x, 32 devices: a whole 2x2x4 slice. The times are simulated.
32 devices in a mesh: space: 8 (over z, y), level: 4 (over x, core).
Axes of the slice: x: 2, y: 2, z: 4, core: 2. Of those that a mesh axis runs over, the one named last changes fastest.
Arguments:
- grid_latent: bfloat16 [4096, 512], P('space'), may hold values from -6 to 6
- mesh_latent: bfloat16 [4, 64, 512], P('level', 'space'), may hold values from -6 to 6
- grid_output_cotangent: bfloat16 [4096, 512], P('space'), may hold values from -6 to 6
- w_send: bfloat16 [512, 512], replicated, may hold values from -0.25 to 0.25
- w_recv: bfloat16 [512, 512], replicated, may hold values from -0.25 to 0.25
- output_weight: bfloat16 [512, 512], replicated, may hold values from -0.25 to 0.25
- hidden_layer_bias: float32 [512], replicated, may hold values from -4 to 4
- output_norm_gain: float32 [512], replicated, may hold values from 0.1 to 1.9
- edge_sender: int32 [4, 16384], P('level', 'space'), may hold values from 0 to 23
- edge_receiver: int32 [4, 16384], P('level', 'space'), may hold values from 0 to 511
- edge_live: int32 [4, 16384], P('level', 'space'), may hold values 0 or 1
Outputs:
- d_grid: float32 [4096, 512], P(('space', 'level'))
- d_mesh: float32 [4, 64, 512], P('level', 'space')
- d_w_send: bfloat16 [512, 512], replicated
- d_w_recv: bfloat16 [512, 512], replicated
- d_w_out: bfloat16 [512, 512], replicated
- d_bias: float32 [512], replicated
- d_gain: float32 [512], replicated
All inputs are finite; a program needn't handle non-finite values. No bound on the sum of `edge_live` on one device may be relied on, other than what follows from the above.
Results may differ from a plain program's by a relative error of at most 0.012.
Values may be sent and summed in bfloat16 or wider, within the bound.
A program may use at most 64 MiB of HBM per device.

v0:
```python
import jax
import jax.numpy as jnp
from jax import lax
from jax.sharding import PartitionSpec as P


def with_halo(cells, sides, width):
    for axis, dim in sides:
        count = lax.axis_size(axis)
        ends = count - 1
        head = lax.slice_in_dim(cells, 0, width, axis=dim)
        tail = lax.slice_in_dim(cells, cells.shape[dim] - width, cells.shape[dim], axis=dim)
        cells = jnp.concatenate(
            [
                lax.ppermute(tail, axis, [(i, (i + 1) % count) for i in range(ends)]),
                cells,
                lax.ppermute(head, axis, [((i + 1) % count, i) for i in range(ends)]),
            ],
            axis=dim,
        )
    return cells


def from_behind(block, axis, distance):
    devices = range(lax.axis_size(axis))
    route = [(i - distance, i) for i in devices if i - distance in devices]
    return lax.ppermute(block, axis, route)


def edge_reverse_step(
    sending_rows,
    receiver_rows,
    cotangent_lines,
    slot_active_flags,
    output_weight,
    hidden_layer_bias,
    output_norm_gain,
):
    preact = sending_rows + receiver_rows + hidden_layer_bias
    hidden = jax.nn.silu(preact).astype(jnp.bfloat16)
    outer = jnp.dot(hidden, output_weight, preferred_element_type=jnp.float32)
    center = outer - jnp.mean(outer, axis=-1, keepdims=True)
    inv_scale = lax.rsqrt(jnp.mean(center * center, axis=-1, keepdims=True) + 1e-05)
    normed = center * inv_scale
    incoming_gradient = cotangent_lines.astype(jnp.float32) * slot_active_flags[:, None].astype(
        jnp.float32
    )
    scaled = incoming_gradient * output_norm_gain
    d_outer = inv_scale * (
        scaled
        - jnp.mean(scaled, axis=-1, keepdims=True)
        - normed * jnp.mean(scaled * normed, axis=-1, keepdims=True)
    )
    d_outer_b = d_outer.astype(jnp.bfloat16)
    w_out_grad = jnp.dot(hidden.T, d_outer_b, preferred_element_type=jnp.float32)
    d_hidden = jnp.dot(d_outer_b, output_weight.T, preferred_element_type=jnp.float32)
    sigmoid = jax.nn.sigmoid(preact)
    preactivation_gradient = d_hidden * sigmoid * (1.0 + preact * (1.0 - sigmoid))
    return (
        preactivation_gradient,
        w_out_grad,
        jnp.sum(preactivation_gradient, axis=0),
        jnp.sum(incoming_gradient * normed, axis=0),
    )


def body(
    grid_latent,
    mesh_latent,
    grid_output_cotangent,
    w_send,
    w_recv,
    output_weight,
    hidden_layer_bias,
    output_norm_gain,
    edge_sender,
    edge_receiver,
    edge_live,
):
    shards = lax.axis_size("space")
    width = grid_latent.shape[1]
    grid_rows = grid_latent.shape[0]
    mesh_rows = mesh_latent.shape[1]
    slots = edge_sender.shape[1]
    sender_local = edge_sender[0]
    receiver_index = edge_receiver[0]
    band = lax.axis_index("space")
    window = sender_local // mesh_rows
    target = band + window - 1
    inside = (target >= 0) & (target < shards)
    window = jnp.where(inside, window, 1)
    table_row = window * mesh_rows + sender_local % mesh_rows
    proj_send = jnp.dot(mesh_latent[0], w_send, preferred_element_type=jnp.float32).astype(
        jnp.bfloat16
    )
    projected_receiver = jnp.dot(grid_latent, w_recv, preferred_element_type=jnp.float32)
    table = with_halo(proj_send, (("space", 0),), mesh_rows)
    sending_rows = table[table_row]
    block = 512
    blocks = slots // block

    def run_block(operands):
        rows_send, rows_recv, rows_cot, rows_live = operands
        return edge_reverse_step(
            rows_send.astype(jnp.float32),
            rows_recv,
            rows_cot,
            rows_live,
            output_weight,
            hidden_layer_bias,
            output_norm_gain,
        )

    operands = (
        sending_rows.reshape(blocks, block, width),
        projected_receiver[receiver_index].reshape(blocks, block, width),
        grid_output_cotangent[receiver_index].reshape(blocks, block, width),
        edge_live[0].reshape(blocks, block),
    )
    d_pre_blocks, wout_blocks, bias_blocks, gain_blocks = lax.map(run_block, operands)
    preactivation_gradient = d_pre_blocks.reshape(slots, width)
    output_weight_piece = jnp.sum(wout_blocks, axis=0)
    bias_piece = jnp.sum(bias_blocks, axis=0)
    gain_piece = jnp.sum(gain_blocks, axis=0)
    table_grads = jax.ops.segment_sum(preactivation_gradient, table_row, num_segments=3 * mesh_rows)
    below = table_grads[:mesh_rows]
    above = table_grads[2 * mesh_rows :]
    from_below = from_behind(above, "space", 1)
    from_above = from_behind(below, "space", -1)
    mesh_acc = table_grads[mesh_rows : 2 * mesh_rows] + from_below + from_above
    grid_local = jax.ops.segment_sum(preactivation_gradient, receiver_index, num_segments=grid_rows)
    share = grid_rows // lax.axis_size("level")
    offset = lax.axis_index("level") * share
    grid_acc = lax.psum_scatter(
        grid_local.astype(jnp.bfloat16), "level", scatter_dimension=0, tiled=True
    )
    grid_part = lax.dynamic_slice_in_dim(grid_latent, offset, share, 0)
    mesh_sum = mesh_acc.astype(jnp.bfloat16)
    d_mesh = jnp.dot(mesh_sum, w_send.T, preferred_element_type=jnp.float32)[None]
    d_grid = jnp.dot(grid_acc, w_recv.T, preferred_element_type=jnp.float32)
    wsend_part = jnp.dot(mesh_latent[0].T, mesh_sum, preferred_element_type=jnp.float32)
    wrecv_part = jnp.dot(grid_part.T, grid_acc, preferred_element_type=jnp.float32)
    totals = lax.psum(
        (wsend_part, wrecv_part, output_weight_piece, bias_piece, gain_piece), ("space", "level")
    )
    d_w_send = totals[0].astype(jnp.bfloat16)
    d_w_recv = totals[1].astype(jnp.bfloat16)
    d_w_out = totals[2].astype(jnp.bfloat16)
    d_bias = totals[3]
    d_gain = totals[4]
    return (d_grid, d_mesh, d_w_send, d_w_recv, d_w_out, d_bias, d_gain)


def solution(mesh):
    return jax.shard_map(
        body,
        mesh=mesh,
        in_specs=(
            P("space", None),
            P("level", "space", None),
            P("space", None),
            P(),
            P(),
            P(),
            P(),
            P(),
            P("level", "space"),
            P("level", "space"),
            P("level", "space"),
        ),
        out_specs=(P(("space", "level"), None), P("level", "space", None), P(), P(), P(), P(), P()),
        check_vma=False,
    )
```

profile of v0, /device:TPU:0, one launch (start us, length us, event | category | flops | bytes accessed | tf_op | source)
XLA Modules:
  0.0 218.6 jit_solution(9644242598406611209)
XLA Ops:
  7.2 1.3 convolution_convert_fusion
  8.5 1.3 collective-permute-start.1
  9.8 5.5 %collective-permute-start = (bf16[8,512]{1,0:T(8,128)(2,1)S(1)}, bf16[8,512]{1,0:T(8,128)(2,1)S(1)}, u32[]{:S(2)}, u32[]{:S(2)}) collective-permute-start(bf16[8,512]{1,0:T(8,128)(2,1)S(1)} %convolution_convert_fusion), channel_id=1, source_target_pairs={{0,4},{4,8},{8,12},{12,16},{16,20},{20,24},{24,28},{1,5},{5,9},{9,... | collective-permute-start | bytes 24584 | tf_op jit(solution)/shard_map/ppermute | solution.py:15
  15.3 0.7 compare_select_fusion
  16.1 0.8 compare_select_fusion.1
  16.9 1.6 fusion.27
  18.5 0.5 broadcast.290
  19.1 1.4 reduce.3
  20.5 9.2 %gather_fusion.2 = bf16[2048,512]{1,0:T(8,128)(2,1)} fusion(bf16[512,512]{1,0:T(8,128)(2,1)S(1)} %copy-done, s32[2048]{0:T(1024)S(1)} %broadcast_clamp_fusion), kind=kCustom, calls=%fused_computation.2 | custom fusion | bytes 4202496 | tf_op jit(solution)/shard_map/gather | solution.py:117
  29.6 8.9 %gather_fusion.1 = f32[2048,512]{1,0:T(8,128)} fusion(f32[512,512]{1,0:T(8,128)S(1)} %fusion.27, s32[2048]{0:T(1024)S(1)} %broadcast_clamp_fusion), kind=kCustom, calls=%fused_computation.1 | custom fusion | bytes 8396800 | tf_op jit(solution)/shard_map/gather | solution.py:116
  38.6 9.2 %gather_fusion = bf16[2048,512]{1,0:T(8,128)(2,1)} fusion(bf16[24,512]{1,0:T(8,128)(2,1)S(1)} %pad_maximum_fusion, s32[2048]{0:T(1024)S(1)} %broadcast_clamp_fusion.1), kind=kCustom, calls=%fused_computation | custom fusion | bytes 4202496 | tf_op jit(solution)/shard_map/gather | solution.py:98
  47.8 37.2 %while.16 = (s32[]{:T(128)}, f32[4,512,512]{2,1,0:T(8,128)}, f32[4,512,512]{2,1,0:T(8,128)}, f32[4,512]{1,0:T(4,128)S(1)}, f32[4,512]{1,0:T(4,128)S(1)}, /*index...) while((s32[]{:T(128)}, f32[4,512,512]{2,1,0:T(8,128)}, ...), condition=%wide.region_7.8_spmd, body=%wide.region_0.7_spmd.sunk | while | flops 816840704 | bytes 18942132 | solution.py:120
  47.8 1.7 multiply_convert_fusion.2
  49.5 1.1 constant_dynamic-slice_fusion.2
  50.5 0.2 copy.24
  50.8 0.5 fusion.60
  51.3 0.2 multiply_reduce_fusion.2
  51.5 0.5 fusion.61
  51.9 0.3 fusion.62
  52.3 1.6 fusion.63
  53.9 3.0 %bitcast_dynamic-update-slice_fusion.2 = (f32[4,512,512]{2,1,0:T(8,128)}, f32[512,512]{1,0:T(8,128)S(1)}) fusion(f32[4,512,512]{2,1,0:T(8,128)} %get-tuple-element.263, s32[]{:T(128)S(6)} %copy.34, f32[512]{0:T(512)S(1)} %get-tuple-element.284, f32[4,512,512]{2,1,0:T(8,128)} %get-tuple-element.283, bf16[4,512,512]{2,1,0:T(8,128)(2,1)} %get-tuple-element.282, ...), kind=kOutput, calls=%fused_computation.20.clone.1 | convolution fusion | flops 271319040 | bytes 4720644 | tf_op jit(solution)/shard_map/while/body/eval_jaxpr/dot_general | solution.py:56
  56.9 0.1 reduce_sum.96
  57.1 1.7 multiply_convert_fusion.2
  58.8 1.1 constant_dynamic-slice_fusion.2
  59.9 0.2 copy.24
  60.1 0.5 fusion.60
  60.6 0.2 multiply_reduce_fusion.2
  60.8 0.5 fusion.61
  61.3 0.3 fusion.62
  61.7 1.5 fusion.63
  63.2 3.1 %bitcast_dynamic-update-slice_fusion.2 = (f32[4,512,512]{2,1,0:T(8,128)}, f32[512,512]{1,0:T(8,128)S(1)}) fusion(f32[4,512,512]{2,1,0:T(8,128)} %get-tuple-element.263, s32[]{:T(128)S(6)} %copy.34, f32[512]{0:T(512)S(1)} %get-tuple-element.284, f32[4,512,512]{2,1,0:T(8,128)} %get-tuple-element.283, bf16[4,512,512]{2,1,0:T(8,128)(2,1)} %get-tuple-element.282, ...), kind=kOutput, calls=%fused_computation.20.clone.1 | convolution fusion | flops 271319040 | bytes 4720644 | tf_op jit(solution)/shard_map/while/body/eval_jaxpr/dot_general | solution.py:56
  66.2 0.1 reduce_sum.96
  66.4 1.7 multiply_convert_fusion.2
  68.1 1.1 constant_dynamic-slice_fusion.2
  69.2 0.2 copy.24
  69.4 0.5 fusion.60
  69.9 0.2 multiply_reduce_fusion.2
  70.1 0.5 fusion.61
  70.6 0.3 fusion.62
  71.0 1.5 fusion.63
  72.5 3.1 %bitcast_dynamic-update-slice_fusion.2 = (f32[4,512,512]{2,1,0:T(8,128)}, f32[512,512]{1,0:T(8,128)S(1)}) fusion(f32[4,512,512]{2,1,0:T(8,128)} %get-tuple-element.263, s32[]{:T(128)S(6)} %copy.34, f32[512]{0:T(512)S(1)} %get-tuple-element.284, f32[4,512,512]{2,1,0:T(8,128)} %get-tuple-element.283, bf16[4,512,512]{2,1,0:T(8,128)(2,1)} %get-tuple-element.282, ...), kind=kOutput, calls=%fused_computation.20.clone.1 | convolution fusion | flops 271319040 | bytes 4720644 | tf_op jit(solution)/shard_map/while/body/eval_jaxpr/dot_general | solution.py:56
  75.5 0.1 reduce_sum.96
  75.7 1.7 multiply_convert_fusion.2
  77.4 1.1 constant_dynamic-slice_fusion.2
  78.5 0.2 copy.24
  78.7 0.5 fusion.60
  79.2 0.2 multiply_reduce_fusion.2
  79.4 0.5 fusion.61
  79.9 0.3 fusion.62
  80.3 1.5 fusion.63
  81.7 3.0 %bitcast_dynamic-update-slice_fusion.2 = (f32[4,512,512]{2,1,0:T(8,128)}, f32[512,512]{1,0:T(8,128)S(1)}) fusion(f32[4,512,512]{2,1,0:T(8,128)} %get-tuple-element.263, s32[]{:T(128)S(6)} %copy.34, f32[512]{0:T(512)S(1)} %get-tuple-element.284, f32[4,512,512]{2,1,0:T(8,128)} %get-tuple-element.283, bf16[4,512,512]{2,1,0:T(8,128)(2,1)} %get-tuple-element.282, ...), kind=kOutput, calls=%fused_computation.20.clone.1 | convolution fusion | flops 271319040 | bytes 4720644 | tf_op jit(solution)/shard_map/while/body/eval_jaxpr/dot_general | solution.py:56
  84.9 13.5 %scatter_custom_fusion = f32[512,512]{1,0:T(8,128)S(1)} fusion(s32[2048]{0:T(1024)} %bitcast.107, f32[2048,512]{1,0:T(8,128)} %bitcast.108, f32[]{:T(128)} %constant.75.clone.1), kind=kCustom, calls=%fused_computation.35 | custom fusion | flops 1048576 | bytes 1049088 | tf_op jit(solution)/shard_map/scatter-add | solution.py:131
  98.4 0.9 convert_element_type.46
  99.3 13.2 %scatter_custom_fusion.1 = f32[24,512]{1,0:T(8,128)S(1)} fusion(s32[2048]{0:T(1024)S(1)} %bitcast.106, f32[2048,512]{1,0:T(8,128)} %bitcast.109, f32[]{:T(128)} %constant.75.clone.1), kind=kCustom, calls=%fused_computation.45 | custom fusion | flops 1048576 | bytes 49664 | tf_op jit(solution)/shard_map/scatter-add | solution.py:125
  112.6 4.8 %collective-permute-start.2 = (f32[8,512]{1,0:T(8,128)S(1)}, f32[8,512]{1,0:T(8,128)S(1)}, u32[]{:S(2)}, u32[]{:S(2)}) collective-permute-start(f32[8,512]{1,0:T(8,128)S(1)} %get-tuple-element.154), channel_id=1, source_target_pairs={{0,4},{4,8},{8,12},{12,16},{16,20},{20,24},{24,28},{1,5},{5,9},{9,... | collective-permute-start | bytes 49160 | tf_op jit(solution)/shard_map/ppermute | solution.py:27
  117.4 1.5 collective-permute-start.3
  118.9 3.8 %reduce_sum.81 = f32[512,512]{1,0:T(8,128)} reduce(f32[4,512,512]{2,1,0:T(8,128)} %get-tuple-element.73, f32[]{:T(128)} %constant.75.clone.1), dimensions={0}, to_apply=%region_13.14 | reduce | flops 786432 | bytes 5242884 | tf_op jit(solution)/shard_map/reduce_sum | solution.py:122
  122.7 0.3 collective-permute-done.3
  123.1 0.3 convolution_bitcast_fusion.1
  123.4 0.9 convolution_bitcast_fusion.2
  124.3 1.3 fusion.14
  125.6 83.1 %all-reduce.2 = (bf16[512,512]{0,1:T(8,128)(2,1)}, bf16[512,512]{1,0:T(8,128)(2,1)}, bf16[512,512]{1,0:T(8,128)(2,1)}, f32[512]{0:T(512)}, f32[512]{0:T(512)}) all-reduce(f32[512,512]{0,1:T(8,128)S(1)} %convolution_bitcast_fusion.1, f32[512,512]{1,0:T(8,128)S(1)} %fusion.14, ...), channel_id=1, replica_groups=mesh['space'=8,'level'=4] {'space','level'}, use_global_device_ids=true, to_apply=%region_11.12 | all-reduce | flops 787456 | bytes 4726784 | tf_op jit(solution)/shard_map/psum | solution.py:143
  208.7 2.0 copy.21
  210.7 1.0 fusion.28
  (59 shorter events, 0.8 us)
Async XLA Ops:
  7.2 13.3 %copy-start = (bf16[512,512]{1,0:T(8,128)(2,1)S(1)}, bf16[512,512]{1,0:T(8,128)(2,1)}, u32[]{:S(2)}) copy-start(bf16[512,512]{1,0:T(8,128)(2,1)} %param.15) | copy-start | bytes 1572868
  7.2 117.1 %reduce-scatter.2.cloned.1.call-start = ((), (), s32[]{:S(2)}) async-start(), calls=%async_computation.1 | async-start | bytes 655360 | tf_op jit(solution)/shard_map/reduce_scatter | solution.py:134
  8.5 30.0 %collective-permute-start.1 = (bf16[8,512]{1,0:T(8,128)(2,1)S(1)}, bf16[8,512]{1,0:T(8,128)(2,1)S(1)}, u32[]{:S(2)}, u32[]{:S(2)}) collective-permute-start(bf16[8,512]{1,0:T(8,128)(2,1)S(1)} %convolution_convert_fusion), channel_id=1, source_target_pairs={{4,0},{8,4},{12,8},{16,12},{20,16},{24,20},{28,24},{5,1},{9,5},{13... | collective-permute-start | bytes 24584 | tf_op jit(solution)/shard_map/ppermute | solution.py:17
  9.8 28.7 %collective-permute-start = (bf16[8,512]{1,0:T(8,128)(2,1)S(1)}, bf16[8,512]{1,0:T(8,128)(2,1)S(1)}, u32[]{:S(2)}, u32[]{:S(2)}) collective-permute-start(bf16[8,512]{1,0:T(8,128)(2,1)S(1)} %convolution_convert_fusion), channel_id=1, source_target_pairs={{0,4},{4,8},{8,12},{12,16},{16,20},{20,24},{24,28},{1,5},{5,9},{9,... | collective-permute-start | bytes 24584 | tf_op jit(solution)/shard_map/ppermute | solution.py:15
  38.5 9.2 %copy-start.1 = (bf16[512,512]{1,0:T(8,128)(2,1)S(1)}, bf16[512,512]{1,0:T(8,128)(2,1)}, u32[]{:S(2)}) copy-start(bf16[512,512]{1,0:T(8,128)(2,1)} %param.18) | copy-start | bytes 1572868
  38.5 9.2 %copy-start.5 = (f32[512]{0:T(512)S(1)}, f32[512]{0:T(512)}, u32[]{:S(2)}) copy-start(f32[512]{0:T(512)} %param.20) | copy-start | bytes 6148
  38.5 9.2 %copy-start.6 = (f32[512]{0:T(512)S(1)}, f32[512]{0:T(512)}, u32[]{:S(2)}) copy-start(f32[512]{0:T(512)} %param.19) | copy-start | bytes 6148
  84.9 38.1 %copy-start.7 = (bf16[1,8,512]{2,1,0:T(8,128)(2,1)S(1)}, bf16[1,8,512]{2,1,0:T(8,128)(2,1)}, u32[]{:S(2)}) copy-start(bf16[1,8,512]{2,1,0:T(8,128)(2,1)} %param.14) | copy-start | bytes 24580
  98.4 25.0 %copy-start.2 = (bf16[512,512]{1,0:T(8,128)(2,1)S(1)}, bf16[512,512]{1,0:T(8,128)(2,1)}, u32[]{:S(2)}) copy-start(bf16[512,512]{1,0:T(8,128)(2,1)} %param.16) | copy-start | bytes 1572868
  112.6 10.1 %collective-permute-start.2 = (f32[8,512]{1,0:T(8,128)S(1)}, f32[8,512]{1,0:T(8,128)S(1)}, u32[]{:S(2)}, u32[]{:S(2)}) collective-permute-start(f32[8,512]{1,0:T(8,128)S(1)} %get-tuple-element.154), channel_id=1, source_target_pairs={{0,4},{4,8},{8,12},{12,16},{16,20},{20,24},{24,28},{1,5},{5,9},{9,... | collective-permute-start | bytes 49160 | tf_op jit(solution)/shard_map/ppermute | solution.py:27
  117.4 5.6 %collective-permute-start.3 = (f32[8,512]{1,0:T(8,128)S(1)}, f32[8,512]{1,0:T(8,128)S(1)}, u32[]{:S(2)}, u32[]{:S(2)}) collective-permute-start(f32[8,512]{1,0:T(8,128)S(1)} %get-tuple-element.155), channel_id=1, source_target_pairs={{4,0},{8,4},{12,8},{16,12},{20,16},{24,20},{28,24},{5,1},{9,5},{13... | collective-permute-start | bytes 49160 | tf_op jit(solution)/shard_map/ppermute | solution.py:27
  122.7 88.0 %copy-start.3 = (bf16[512,512]{1,0:T(8,128)(2,1)S(1)}, bf16[512,512]{1,0:T(8,128)(2,1)}, u32[]{:S(2)}) copy-start(bf16[512,512]{1,0:T(8,128)(2,1)} %param.17) | copy-start | bytes 1572868
  124.3 86.5 %copy-start.4 = (bf16[128,512]{1,0:T(8,128)(2,1)S(1)}, bf16[128,512]{1,0:T(8,128)(2,1)}, u32[]{:S(2)}) copy-start(bf16[128,512]{1,0:T(8,128)(2,1)} %reduce-scatter.2.cloned.1.call-done) | copy-start | bytes 393220
Sparse Core Ops, SparseCore 0:
  99.4 23.2 reduce-scatter.1
where the time goes:
time: 220 us; the launch traced here: 219 us
  blocking collectives  83.1 us (38%)
  other arithmetic  45.5 us (21%)
  local copies, waits for them, and re-layouts  35.4 us (16%)
  matrix products  26.6 us (12%)
  between operations  14.3 us (6%)
  starting transfers between devices  13.2 us (6%)
    psum x1, blocking collectives, body(): lax.psum((wsend_part, wrecv_part, output_weight_piece, bias_piece, gain_p...  83.1 us
    scatter-add x1, other arithmetic, body(): jax.ops.segment_sum(preactivation_gradient, receiver_index, num_segments=...  13.5 us
    scatter-add x1, other arithmetic, body(): jax.ops.segment_sum(preactivation_gradient, table_row, num_segments=3 * m...  13.2 us
    dot_general x4, matrix products, edge_reverse_step(): jnp.dot(d_outer_b, output_weight.T, preferred_element_type=jnp.float32)  12.2 us
    gather x1, local copies, waits for them, and re-layouts, body(): sending_rows = table[table_row]  9.18 us
    gather x1, local copies, waits for them, and re-layouts, body(): grid_output_cotangent[receiver_index].reshape(blocks, block, width)  9.15 us
    gather x1, local copies, waits for them, and re-layouts, body(): projected_receiver[receiver_index].reshape(blocks, block, width)  8.9 us
    convert_element_type x4, other arithmetic, edge_reverse_step(): hidden = jax.nn.silu(preact).astype(jnp.bfloat16)  6.68 us
  transfers between devices with their start and end apart: 5, of which 1 were waited for; matrix products, arithmetic and copies ran while one was open for 19% of the time, Pallas kernels for 0%

commit v1 on v0

v1 whole, which is shorter than its diff:
```python
import functools

import jax
import jax.numpy as jnp
from jax import lax
from jax.experimental import pallas as pl
from jax.experimental.pallas import tpu as pltpu
from jax.sharding import PartitionSpec as P

MESH = pl.DeviceIdType.MESH
F32 = jnp.float32
BF16 = jnp.bfloat16
TILE = 16


def mm(a, b, ca=1, cb=0):
    return lax.dot_general(a, b, (((ca,), (cb,)), ((), ())), preferred_element_type=F32)


def bit_steps(axis, count):
    steps = []
    width = 1
    while width < count:
        steps.append((axis, width))
        width *= 2
    return steps


def partner(axis, width):
    me = lax.axis_index(axis)
    bit = (me // width) % 2
    return bit, {axis: me + (1 - 2 * bit) * width}


def halvings(rows, steps):
    plan = []
    size = rows
    for axis, width in steps:
        split = (size // 2) % TILE == 0
        plan.append((axis, width, size, split))
        if split:
            size //= 2
    return plan, size


def reversed_chunks(count):
    order = [0]
    width = 1
    while width < count:
        order = [2 * c for c in order] + [2 * c + 1 for c in order]
        width *= 2
    return order


def kernel(
    n_space,
    n_level,
    block,
    grid_ref,
    mesh_ref,
    cot_ref,
    wsend_ref,
    wrecv_ref,
    wout_ref,
    bias_ref,
    gain_ref,
    snd_ref,
    rcv_ref,
    live_ref,
    dgrid_ref,
    dmesh_ref,
    dw_ref,
    dvec_ref,
    window,
    table,
    proj,
    wacc,
    gacc,
    macc,
    vacc,
    red,
    red_in,
    gbuf,
    gbuf_in,
    vec,
    vec_in,
    mout,
    m_in,
    halo_sem,
    mgrad_sem,
    red_sem,
    gat_sem,
    grid_sem,
    vec_sem,
):
    rows, width = grid_ref.shape
    mrows = mesh_ref.shape[0]
    slots = snd_ref.shape[1]
    band = lax.axis_index("space")
    steps = bit_steps("level", n_level) + bit_steps("space", n_space)
    first = band > 0
    last = band < n_space - 1
    pad = table.shape[0]

    window[...] = jnp.zeros_like(window)
    macc[...] = jnp.zeros_like(macc)
    m_in[...] = jnp.zeros_like(m_in)
    barrier = pltpu.get_barrier_semaphore()
    for axis, w in steps:
        _, who = partner(axis, w)
        pl.semaphore_signal(barrier, inc=1, device_id=who, device_id_type=MESH)
    up = {"space": (band + 1) % n_space}
    down = {"space": (band + n_space - 1) % n_space}
    pl.semaphore_signal(barrier, inc=1, device_id=up, device_id_type=MESH)
    pl.semaphore_signal(barrier, inc=1, device_id=down, device_id_type=MESH)
    pl.semaphore_wait(barrier, len(steps) + 2)

    def remote(src, dst, sem, who):
        return pltpu.make_async_remote_copy(
            src_ref=src,
            dst_ref=dst,
            send_sem=sem.at[0],
            recv_sem=sem.at[1],
            device_id=who,
            device_id_type=MESH,
        )

    to_up = remote(mesh_ref, window.at[0], halo_sem.at[0], up)
    to_down = remote(mesh_ref, window.at[2], halo_sem.at[1], down)

    @pl.when(last)
    def _():
        to_up.start()

    @pl.when(first)
    def _():
        to_down.start()

    window[1] = mesh_ref[...]
    proj[...] = mm(grid_ref[...], wrecv_ref[...]).astype(BF16)
    wacc[...] = jnp.zeros_like(wacc)
    gacc[...] = jnp.zeros_like(gacc)
    vacc[...] = jnp.zeros_like(vacc)

    @pl.when(last)
    def _():
        to_up.wait_send()
        to_down.wait_recv()

    @pl.when(first)
    def _():
        to_down.wait_send()
        to_up.wait_recv()

    win = jnp.concatenate(
        [window[k].astype(F32) for k in range(3)] + [jnp.zeros((pad - 3 * mrows, width), F32)], axis=0
    ).astype(BF16)
    table[...] = mm(win, wsend_ref[...]).astype(BF16)

    def step(i, _):
        at = pl.ds(pl.multiple_of(i * block, block), block)
        snd = snd_ref[:, at]
        rcv = rcv_ref[:, at]
        live = live_ref[:, at]
        slot = snd // mrows
        target = band + slot - 1
        slot = jnp.where((target >= 0) & (target < n_space), slot, 1)
        src = slot * mrows + snd % mrows

        def column(v):
            return jnp.transpose(jnp.broadcast_to(v, (128, block)))

        rcv_c = column(rcv)
        src_c = column(src)
        live_c = column(live.astype(F32))
        reps = rows // 128
        wreps = width // 128
        pick = (
            jnp.concatenate([rcv_c] * reps, axis=1)
            == lax.broadcasted_iota(jnp.int32, (block, rows), 1)
        ).astype(F32).astype(BF16)
        pick_s = (
            jnp.concatenate([src_c] * (pad // 128), axis=1)
            == lax.broadcasted_iota(jnp.int32, (block, pad), 1)
        ).astype(F32).astype(BF16)
        put = (
            jnp.broadcast_to(rcv, (rows, block))
            == lax.broadcasted_iota(jnp.int32, (rows, block), 0)
        ).astype(F32).astype(BF16)
        put_s = (
            jnp.broadcast_to(src, (macc.shape[0], block))
            == lax.broadcasted_iota(jnp.int32, (macc.shape[0], block), 0)
        ).astype(F32).astype(BF16)

        preact = mm(pick, proj[...]) + mm(pick_s, table[...]) + bias_ref[...]
        sig = jax.nn.sigmoid(preact)
        hidden = (preact * sig).astype(BF16)
        outer = mm(hidden, wout_ref[...])
        center = outer - jnp.mean(outer, axis=-1, keepdims=True)
        inv = lax.rsqrt(jnp.mean(center * center, axis=-1, keepdims=True) + 1e-05)
        normed = center * inv
        upstream = mm(pick, cot_ref[...]) * jnp.concatenate([live_c] * wreps, axis=1)
        scaled = upstream * gain_ref[...]
        d_outer = inv * (
            scaled
            - jnp.mean(scaled, axis=-1, keepdims=True)
            - normed * jnp.mean(scaled * normed, axis=-1, keepdims=True)
        )
        d_outer = d_outer.astype(BF16)
        wacc[...] += mm(hidden, d_outer, 0, 0)
        d_pre = mm(d_outer, wout_ref[...], 1, 1) * (sig * (1.0 + preact * (1.0 - sig)))
        vacc[0] += jnp.sum(d_pre.reshape(block // 8, 8, width), axis=0)
        vacc[1] += jnp.sum((upstream * normed).reshape(block // 8, 8, width), axis=0)
        d_pre = d_pre.astype(BF16)
        gacc[...] += mm(put, d_pre)
        macc[...] += mm(put_s, d_pre)
        return 0

    lax.fori_loop(0, slots // block, step, 0)

    mout[0] = macc[0:mrows]
    mout[1] = macc[2 * mrows : 3 * mrows]
    g_up = remote(mout.at[1], m_in.at[0], mgrad_sem.at[0], up)
    g_down = remote(mout.at[0], m_in.at[1], mgrad_sem.at[1], down)

    @pl.when(last)
    def _():
        g_up.start()

    @pl.when(first)
    def _():
        g_down.start()

    vec[0] = jnp.concatenate(
        [jnp.sum(vacc[k], axis=0, keepdims=True) for k in range(2)], axis=0
    )
    share = rows // n_level
    for place, chunk in enumerate(reversed_chunks(n_level)):
        gbuf[place * share : (place + 1) * share] = gacc[chunk * share : (chunk + 1) * share].astype(BF16)
    red[0:width] = wacc[...].astype(BF16)
    red[width : 2 * width] = mm(grid_ref[...], gacc[...].astype(BF16), 0, 0).astype(BF16)
    red[2 * width : 3 * width] = mm(win, jnp.concatenate(
        [macc[0 : 3 * mrows], jnp.zeros((pad - 3 * mrows, width), F32)], axis=0
    ).astype(BF16), 0, 0).astype(BF16)

    plan, _ = halvings(red.shape[0], steps)
    off = 0
    goff = 0
    gsize = rows
    spot = 0
    trail = []
    for k, (axis, w, size, split) in enumerate(plan):
        bit, who = partner(axis, w)
        half = size // 2 if split else size
        give = off + (1 - bit) * half if split else off
        keep = off + bit * half if split else off
        at_give = pl.ds(pl.multiple_of(give, TILE), half)
        at_keep = pl.ds(pl.multiple_of(keep, TILE), half)
        into = red_in.at[pl.ds(spot, half)]
        copies = [
            remote(red.at[at_give], into, red_sem.at[k], who),
            remote(vec.at[k], vec_in.at[k], vec_sem.at[k], who),
        ]
        if axis == "level":
            gsize //= 2
            g_give = pl.ds(pl.multiple_of(goff + (1 - bit) * gsize, TILE), gsize)
            g_keep = pl.ds(pl.multiple_of(goff + bit * gsize, TILE), gsize)
            g_into = gbuf_in.at[pl.ds(rows - 2 * gsize, gsize)]
            copies.append(remote(gbuf.at[g_give], g_into, grid_sem.at[k], who))
            goff = goff + bit * gsize
        for c in copies:
            c.start()
        for c in copies:
            c.wait()
        red[at_keep] = (red[at_keep].astype(F32) + red_in[pl.ds(spot, half)].astype(F32)).astype(BF16)
        vec[k + 1] = vec[k] + vec_in[k]
        if axis == "level":
            gbuf[g_keep] = (
                gbuf[g_keep].astype(F32) + gbuf_in[pl.ds(rows - 2 * gsize, gsize)].astype(F32)
            ).astype(BF16)
        spot += half
        if split:
            trail.append((k, who, half))
        off = keep
    dvec_ref[...] = vec[len(plan)]

    held = trail[-1][2]
    at = pl.ds(pl.multiple_of(off, TILE), held)
    dw_ref[at] = red[at]
    for k, who, half in reversed(trail):
        at = pl.ds(pl.multiple_of(off, TILE), half)
        c = remote(dw_ref.at[at], dw_ref.at[at], gat_sem.at[k], who)
        c.start()
        if k == trail[-1][0]:
            g_at = pl.ds(pl.multiple_of(goff, TILE), share)
            dgrid_ref[...] = mm(gbuf[g_at], wrecv_ref[...], 1, 1)

            @pl.when(last)
            def _():
                g_up.wait_send()
                g_down.wait_recv()

            @pl.when(first)
            def _():
                g_down.wait_send()
                g_up.wait_recv()

            total = macc[mrows : 2 * mrows] + m_in[0] + m_in[1]
            total = jnp.concatenate([total, jnp.zeros((TILE - mrows % TILE, width), F32)], axis=0)
            dmesh_ref[...] = mm(total.astype(BF16), wsend_ref[...], 1, 1)[0:mrows]
        c.wait()
        off = off - ((off // half) % 2) * half


def body(
    grid_latent,
    mesh_latent,
    grid_output_cotangent,
    w_send,
    w_recv,
    output_weight,
    hidden_layer_bias,
    output_norm_gain,
    edge_sender,
    edge_receiver,
    edge_live,
):
    n_space = lax.axis_size("space")
    n_level = lax.axis_size("level")
    rows, width = grid_latent.shape
    mrows = mesh_latent.shape[1]
    slots = edge_sender.shape[1]
    block = min(256, slots)
    pad = -(-3 * mrows // 128) * 128
    mpad = -(-3 * mrows // TILE) * TILE
    steps = bit_steps("level", n_level) + bit_steps("space", n_space)
    n = len(steps)
    plan, _ = halvings(3 * width, steps)
    inbox = sum(size // 2 if split else size for _, _, size, split in plan)
    vm = pl.BlockSpec(memory_space=pltpu.VMEM)
    dma = pltpu.SemaphoreType.DMA
    d_grid, d_mesh, d_w, d_vec = pl.pallas_call(
        functools.partial(kernel, n_space, n_level, block),
        out_shape=(
            jax.ShapeDtypeStruct((rows // n_level, width), F32),
            jax.ShapeDtypeStruct((mrows, width), F32),
            jax.ShapeDtypeStruct((3 * width, width), BF16),
            jax.ShapeDtypeStruct((2, width), F32),
        ),
        in_specs=[vm] * 11,
        out_specs=(vm,) * 4,
        scratch_shapes=[
            pltpu.VMEM((3, mrows, width), BF16),
            pltpu.VMEM((pad, width), BF16),
            pltpu.VMEM((rows, width), BF16),
            pltpu.VMEM((width, width), F32),
            pltpu.VMEM((rows, width), F32),
            pltpu.VMEM((mpad, width), F32),
            pltpu.VMEM((2, 8, width), F32),
            pltpu.VMEM((3 * width, width), BF16),
            pltpu.VMEM((inbox, width), BF16),
            pltpu.VMEM((rows, width), BF16),
            pltpu.VMEM((rows, width), BF16),
            pltpu.VMEM((n + 1, 2, width), F32),
            pltpu.VMEM((n, 2, width), F32),
            pltpu.VMEM((2, mrows, width), F32),
            pltpu.VMEM((2, mrows, width), F32),
            dma((2, 2)),
            dma((2, 2)),
            dma((n, 2)),
            dma((n, 2)),
            dma((n, 2)),
            dma((n, 2)),
        ],
        compiler_params=pltpu.CompilerParams(collective_id=0, has_side_effects=True),
        name="edge_backward",
    )(
        grid_latent,
        mesh_latent[0],
        grid_output_cotangent,
        w_send,
        w_recv,
        output_weight,
        hidden_layer_bias[None],
        output_norm_gain[None],
        edge_sender,
        edge_receiver,
        edge_live,
    )
    return (
        d_grid,
        d_mesh[None],
        d_w[2 * width :],
        d_w[width : 2 * width],
        d_w[:width],
        d_vec[0],
        d_vec[1],
    )


def solution(mesh):
    return jax.shard_map(
        body,
        mesh=mesh,
        in_specs=(
            P("space", None),
            P("level", "space", None),
            P("space", None),
            P(),
            P(),
            P(),
            P(),
            P(),
            P("level", "space"),
            P("level", "space"),
            P("level", "space"),
        ),
        out_specs=(P(("space", "level"), None), P("level", "space", None), P(), P(), P(), P(), P()),
        check_vma=False,
    )
```

time: 220 us -> 82.8 us (0.38)
  blocking collectives: 83.1 us -> 0 us
  Pallas kernels: 0 us -> 76.7 us
  other arithmetic: 45.5 us -> 0 us
  local copies, waits for them, and re-layouts: 35.4 us -> 5.22 us
  matrix products: 26.6 us -> 0 us
  between operations: 14.3 us -> 0.65 us
  starting transfers between devices: 13.2 us -> 0 us
    psum x1 -> x0, blocking collectives: 83.1 us -> none  [body(): lax.psum((wsend_part, wrecv_part, output_weight_piece, bias_piece, gain_p...]
    pallas_call x0 -> x1, Pallas kernels: none -> 76.7 us  [body(): pl.pallas_call(functools.partial(kernel, n_space, n_level, block), out_sh...]
    gather x3 -> x0, local copies, waits for them, and re-layouts: 27.2 us -> none  [the longest x1 9.18 us: body(): sending_rows = table[table_row]]
    scatter-add x2 -> x0, other arithmetic: 26.7 us -> none  [the longest x1 13.5 us: body(): jax.ops.segment_sum(preactivation_gradient, receiver_index, num_segments=...]
    dot_general x18 -> x0, matrix products: 26.6 us -> none  [the longest x4 12.2 us: edge_reverse_step(): jnp.dot(d_outer_b, output_weight.T, preferred_element_type=jnp.float32)]
    ppermute x4 -> x0, starting transfers between devices: 13.1 us -> none  [the longest x2 6.29 us: from_behind(): return lax.ppermute(block, axis, route)]
    convert_element_type x14 -> x0, other arithmetic: 9 us -> none  [the longest x4 6.68 us: edge_reverse_step(): hidden = jax.nn.silu(preact).astype(jnp.bfloat16)]
    reduce_sum x15 -> x0, other arithmetic: 6.81 us -> none  [the longest x1 3.77 us: body(): output_weight_piece = jnp.sum(wout_blocks, axis=0)]
  transfers between devices with their start and end apart: 5 -> 0, of which waited for: 1 -> 0; matrix products, arithmetic and copies ran while one was open for 19% -> 0% of each run, Pallas kernels for 0% -> 0%
where the time goes in v1:
time: 82.8 us; the launch traced here: 82.6 us
  Pallas kernels  76.7 us (93%)
  local copies, waits for them, and re-layouts  5.22 us (6%)
    pallas_call x1, Pallas kernels, body(): pl.pallas_call(functools.partial(kernel, n_space, n_level, block), out_sh...  76.7 us
    slice x1, local copies, waits for them, and re-layouts, body(): d_w[:width]  2.57 us

profile of v1, /device:TPU:0, one launch (start us, length us, event | category | flops | bytes accessed | tf_op | source)
XLA Modules:
  0.0 82.6 jit_solution(6491108043304566168)
XLA Ops:
  0.6 76.7 %edge_backward.1 = (f32[128,512]{1,0:T(8,128)}, f32[8,512]{1,0:T(8,128)}, bf16[1536,512]{1,0:T(8,128)(2,1)}, f32[2,512]{1,0:T(2,128)}) custom-call(bf16[512,512]{1,0:T(8,128)(2,1)} %grid_ref.1, bf16[8,512]{1,0:T(8,128)(2,1)} %bitcast.7, bf16[512,512]{1,0:T(8,128)(2,1)} %cot_ref.1, bf16[512,512]{1,0:T(8,128)(2,1)} %wsend_ref.1, bf16[512,512]{1,0:T(8,128)(2,1)} %wrecv_ref.1, ...), custom_call_target="tpu_custom_call" | custom-call | tf_op jit(solution)/shard_map/edge_backward/pallas_call | solution.py:342
  77.3 1.3 %fusion.1 = (f32[1,512]{1,0:T(1,128)}, f32[1,512]{1,0:T(1,128)}) fusion(f32[2,512]{1,0:T(2,128)} %get-tuple-element.14), kind=kLoop, calls=%fused_computation.1 | loop fusion | bytes 8192 | tf_op jit(solution)/shard_map/slice | solution.py:397
  78.7 0.0 copy-start
  78.7 0.0 copy-start.1
  78.7 2.6 %fusion = (bf16[512,512]{1,0:T(8,128)(2,1)}, bf16[512,512]{1,0:T(8,128)(2,1)}, bf16[512,512]{1,0:T(8,128)(2,1)}) fusion(bf16[1536,512]{1,0:T(8,128)(2,1)} %get-tuple-element.13), kind=kLoop, calls=%fused_computation | loop fusion | bytes 3145728 | tf_op jit(solution)/shard_map/slice | solution.py:395
  81.2 0.0 copy-done
  81.2 0.7 copy.20
  82.0 0.0 copy-done.1
  82.0 0.6 copy.21
Async XLA Ops:
  78.7 2.6 %copy-start = (f32[128,512]{1,0:T(8,128)S(1)}, f32[128,512]{1,0:T(8,128)}, u32[]{:S(2)}) copy-start(f32[128,512]{1,0:T(8,128)} %get-tuple-element.27) | copy-start | bytes 786436
  78.7 3.3 %copy-start.1 = (f32[8,512]{1,0:T(8,128)S(1)}, f32[8,512]{1,0:T(8,128)}, u32[]{:S(2)}) copy-start(f32[8,512]{1,0:T(8,128)} %get-tuple-element.12) | copy-start | bytes 49156

commit v2 on v1

v2 whole, which is shorter than its diff:
```python
import functools

import jax
import jax.numpy as jnp
from jax import lax
from jax.experimental import pallas as pl
from jax.experimental.pallas import tpu as pltpu
from jax.sharding import PartitionSpec as P

MESH = pl.DeviceIdType.MESH
F32 = jnp.float32
BF16 = jnp.bfloat16
TILE = 16


def mm(a, b, ca=1, cb=0):
    return lax.dot_general(a, b, (((ca,), (cb,)), ((), ())), preferred_element_type=F32)


def bit_steps(axis, count):
    steps = []
    width = 1
    while width < count:
        steps.append((axis, width))
        width *= 2
    return steps


def partner(axis, width):
    me = lax.axis_index(axis)
    bit = (me // width) % 2
    return bit, {axis: me + (1 - 2 * bit) * width}


def reversed_chunks(count):
    order = [0]
    width = 1
    while width < count:
        order = [2 * c for c in order] + [2 * c + 1 for c in order]
        width *= 2
    return order


def step_orders(n_space, n_level):
    level = bit_steps("level", n_level)
    space = bit_steps("space", n_space)
    return level + space, level[:-1] + space[:1] + level[-1:] + space[1:]


def halvings(rows, steps):
    plan = []
    size = rows
    for axis, width in steps:
        split = (size // 2) % TILE == 0
        plan.append((axis, width, size, split))
        if split:
            size //= 2
    return plan


def inbox_rows(rows, steps):
    return sum(size // 2 if split else size for _, _, size, split in halvings(rows, steps))


def remote(src, dst, sem, who):
    return pltpu.make_async_remote_copy(
        src_ref=src,
        dst_ref=dst,
        send_sem=sem.at[0],
        recv_sem=sem.at[1],
        device_id=who,
        device_id_type=MESH,
    )


def reduce_lane(buf, out, inbox, cols, sem_r, sem_g, steps):
    off = 0
    spot = 0
    trail = []
    for k, (axis, w, size, split) in enumerate(halvings(buf.shape[0], steps)):
        bit, who = partner(axis, w)
        half = size // 2 if split else size
        give = off + (1 - bit) * half if split else off
        keep = off + bit * half if split else off
        at_give = pl.ds(pl.multiple_of(give, TILE), half)
        at_keep = pl.ds(pl.multiple_of(keep, TILE), half)
        into = pl.ds(spot, half)
        c = remote(buf.at[at_give, cols], inbox.at[into], sem_r.at[k], who)
        c.start()
        yield
        c.wait()
        buf[at_keep, cols] = (buf[at_keep, cols].astype(F32) + inbox[into].astype(F32)).astype(BF16)
        spot += half
        off = keep
        if split:
            trail.append((k, who, half, bit))
    at = pl.ds(pl.multiple_of(off, TILE), trail[-1][2])
    out[at, cols] = buf[at, cols]
    for k, who, half, bit in reversed(trail):
        at = pl.ds(pl.multiple_of(off, TILE), half)
        c = remote(out.at[at, cols], out.at[at, cols], sem_g.at[k], who)
        c.start()
        yield
        c.wait()
        off = off - bit * half


def gather_lane(buf, sem, steps):
    base = gather_place(steps)
    for j, (axis, w) in enumerate(reversed(steps)):
        bit, who = partner(axis, w)
        at = pl.ds(base, 1 << j)
        c = remote(buf.at[at], buf.at[at], sem.at[j], who)
        c.start()
        yield
        c.wait()
        base = base - bit * (1 << j)


def gather_place(steps):
    place = 0
    for j, (axis, w) in enumerate(reversed(steps)):
        place = place + partner(axis, w)[0] * (1 << j)
    return place


def grid_lane(gbuf, inbox, dgrid_ref, wrecv_ref, sem, n_level):
    off = 0
    size = gbuf.shape[0]
    spot = 0
    for k, (axis, w) in enumerate(bit_steps("level", n_level)):
        bit, who = partner(axis, w)
        size //= 2
        give = pl.ds(pl.multiple_of(off + (1 - bit) * size, TILE), size)
        keep = pl.ds(pl.multiple_of(off + bit * size, TILE), size)
        into = pl.ds(spot, size)
        c = remote(gbuf.at[give], inbox.at[into], sem.at[k], who)
        c.start()
        yield
        c.wait()
        gbuf[keep] = (gbuf[keep].astype(F32) + inbox[into].astype(F32)).astype(BF16)
        spot += size
        off = off + bit * size
    dgrid_ref[...] = mm(gbuf[pl.ds(pl.multiple_of(off, TILE), size)], wrecv_ref[...], 1, 1)


def vec_lane(vec, inbox, dvec_ref, sem, steps):
    for k, (axis, w) in enumerate(steps):
        _, who = partner(axis, w)
        c = remote(vec.at[k], inbox.at[k], sem.at[k], who)
        c.start()
        yield
        c.wait()
        vec[k + 1] = vec[k] + inbox[k]
    dvec_ref[...] = vec[len(steps)]


def edge_copies(up, down):
    n_space = lax.axis_size("space")
    band = lax.axis_index("space")
    first = band > 0
    last = band < n_space - 1

    def start():
        @pl.when(last)
        def _():
            up.start()

        @pl.when(first)
        def _():
            down.start()

    def wait():
        @pl.when(last)
        def _():
            up.wait_send()
            down.wait_recv()

        @pl.when(first)
        def _():
            down.wait_send()
            up.wait_recv()

    return start, wait


def advance(lanes):
    for lane in list(lanes):
        if next(lane, "end") == "end":
            lanes.remove(lane)


def kernel(
    n_space,
    n_level,
    block,
    segments,
    grid_ref,
    mesh_ref,
    cot_ref,
    wsend_ref,
    wrecv_ref,
    wout_ref,
    bias_ref,
    gain_ref,
    snd_ref,
    rcv_ref,
    live_ref,
    dgrid_ref,
    dmesh_ref,
    dwo_ref,
    dwr_ref,
    dws_ref,
    dvec_ref,
    window,
    table,
    proj,
    pre,
    ups,
    dout,
    wacc,
    gacc,
    macc,
    vacc,
    red_o,
    red_r,
    inbox,
    gbuf,
    gbuf_in,
    vec,
    vec_in,
    mout,
    m_in,
    mesh_all,
    sum_all,
    halo_sem,
    mgrad_sem,
    red_sem,
    gat_sem,
    mesh_sem,
    grid_sem,
    vec_sem,
):
    rows, width = grid_ref.shape
    mrows = mesh_ref.shape[0]
    slots = snd_ref.shape[1]
    band = lax.axis_index("space")
    steps, swapped = step_orders(n_space, n_level)
    pad = table.shape[0]

    window[...] = jnp.zeros_like(window)
    m_in[...] = jnp.zeros_like(m_in)
    barrier = pltpu.get_barrier_semaphore()
    for axis, w in steps:
        _, who = partner(axis, w)
        pl.semaphore_signal(barrier, inc=1, device_id=who, device_id_type=MESH)
    up = {"space": (band + 1) % n_space}
    down = {"space": (band + n_space - 1) % n_space}
    pl.semaphore_signal(barrier, inc=1, device_id=up, device_id_type=MESH)
    pl.semaphore_signal(barrier, inc=1, device_id=down, device_id_type=MESH)
    macc[...] = jnp.zeros_like(macc)
    wacc[...] = jnp.zeros_like(wacc)
    gacc[...] = jnp.zeros_like(gacc)
    vacc[...] = jnp.zeros_like(vacc)
    window[1] = mesh_ref[...]
    place = gather_place(steps)
    mesh_all[place] = mesh_ref[...]
    proj[...] = mm(grid_ref[...], wrecv_ref[...]).astype(BF16)
    pl.semaphore_wait(barrier, len(steps) + 2)

    halo_start, halo_wait = edge_copies(
        remote(mesh_ref, window.at[0], halo_sem.at[0], up),
        remote(mesh_ref, window.at[2], halo_sem.at[1], down),
    )
    halo_start()
    early = [gather_lane(mesh_all, mesh_sem.at[0], steps)]
    advance(early)

    def span(i):
        return pl.ds(pl.multiple_of(i * block, block), block)

    def column(v):
        return jnp.transpose(jnp.broadcast_to(v, (128, block)))

    def one_hot(hit):
        return hit.astype(F32).astype(BF16)

    def source(at):
        snd = snd_ref[:, at]
        slot = snd // mrows
        target = band + slot - 1
        slot = jnp.where((target >= 0) & (target < n_space), slot, 1)
        return slot * mrows + snd % mrows

    def gathers(i, _):
        at = span(i)
        rcv_c = column(rcv_ref[:, at])
        live_c = column(live_ref[:, at].astype(F32))
        pick = one_hot(
            jnp.concatenate([rcv_c] * (rows // 128), axis=1)
            == lax.broadcasted_iota(jnp.int32, (block, rows), 1)
        )
        pre[at] = mm(pick, proj[...]) + bias_ref[...]
        ups[at] = (mm(pick, cot_ref[...]) * jnp.concatenate([live_c] * (width // 128), axis=1)).astype(BF16)
        return 0

    count = slots // block
    lax.fori_loop(0, count, gathers, 0)

    halo_wait()
    win = jnp.concatenate(
        [window[k].astype(F32) for k in range(3)] + [jnp.zeros((pad - 3 * mrows, width), F32)], axis=0
    ).astype(BF16)
    table[...] = mm(win, wsend_ref[...]).astype(BF16)

    def forward(i, _):
        at = span(i)
        src_c = column(source(at))
        pick = one_hot(
            jnp.concatenate([src_c] * (pad // 128), axis=1)
            == lax.broadcasted_iota(jnp.int32, (block, pad), 1)
        )
        preact = pre[at] + mm(pick, table[...])
        sig = jax.nn.sigmoid(preact)
        hidden = (preact * sig).astype(BF16)
        pre[at] = sig * (1.0 + preact * (1.0 - sig))
        outer = mm(hidden, wout_ref[...])
        center = outer - jnp.mean(outer, axis=-1, keepdims=True)
        inv = lax.rsqrt(jnp.mean(center * center, axis=-1, keepdims=True) + 1e-05)
        normed = center * inv
        upstream = ups[at].astype(F32)
        scaled = upstream * gain_ref[...]
        d_outer = inv * (
            scaled
            - jnp.mean(scaled, axis=-1, keepdims=True)
            - normed * jnp.mean(scaled * normed, axis=-1, keepdims=True)
        )
        d_outer = d_outer.astype(BF16)
        dout[at] = d_outer
        wacc[...] += mm(hidden, d_outer, 0, 0)
        vacc[1] += jnp.sum((upstream * normed).reshape(block // 8, 8, width), axis=0)
        return 0

    def backward(i, _):
        at = span(i)
        put = one_hot(
            jnp.broadcast_to(rcv_ref[:, at], (rows, block))
            == lax.broadcasted_iota(jnp.int32, (rows, block), 0)
        )
        put_s = one_hot(
            jnp.broadcast_to(source(at), (macc.shape[0], block))
            == lax.broadcasted_iota(jnp.int32, (macc.shape[0], block), 0)
        )
        d_pre = mm(dout[at], wout_ref[...], 1, 1) * pre[at]
        vacc[0] += jnp.sum(d_pre.reshape(block // 8, 8, width), axis=0)
        d_pre = d_pre.astype(BF16)
        gacc[...] += mm(put, d_pre)
        macc[...] += mm(put_s, d_pre)
        return 0

    cuts = [count * k // segments for k in range(segments + 1)]
    for lo, hi in zip(cuts, cuts[1:]):
        lax.fori_loop(lo, hi, forward, 0)
        advance(early)

    half = width // 2
    sides = [(pl.ds(0, half), steps), (pl.ds(half, half), swapped)]

    def reducers(buf, out, at):
        return [
            reduce_lane(buf, out, inbox.at[at + k], cols, red_sem.at[at + k], gat_sem.at[at + k], order)
            for k, (cols, order) in enumerate(sides)
        ]

    red_o[...] = wacc[...].astype(BF16)
    out_lanes = reducers(red_o, dwo_ref, 0) + early
    advance(out_lanes)
    for lo, hi in zip(cuts, cuts[1:]):
        lax.fori_loop(lo, hi, backward, 0)
        if hi < count:
            advance(out_lanes)

    red_r[...] = mm(grid_ref[...], gacc[...].astype(BF16), 0, 0).astype(BF16)
    lanes = reducers(red_r, dwr_ref, 2)
    advance(lanes)

    def mesh_lane():
        mout[0] = macc[0:mrows]
        mout[1] = macc[2 * mrows : 3 * mrows]
        start, wait = edge_copies(
            remote(mout.at[1], m_in.at[0], mgrad_sem.at[0], up),
            remote(mout.at[0], m_in.at[1], mgrad_sem.at[1], down),
        )
        start()
        yield
        wait()
        total = macc[mrows : 2 * mrows] + m_in[0] + m_in[1]
        sum_all[place] = total.astype(BF16)
        lane = gather_lane(sum_all, mesh_sem.at[1], steps)
        next(lane)
        total = jnp.concatenate([total, jnp.zeros((TILE - mrows % TILE, width), F32)], axis=0)
        dmesh_ref[...] = mm(total.astype(BF16), wsend_ref[...], 1, 1)[0:mrows]
        yield
        yield from lane
        every = mesh_all.shape[0] * mrows
        dws_ref[...] = mm(
            mesh_all[...].astype(F32).reshape(every, width).astype(BF16),
            sum_all[...].astype(F32).reshape(every, width).astype(BF16),
            0,
            0,
        ).astype(BF16)

    share = rows // n_level
    for spot, chunk in enumerate(reversed_chunks(n_level)):
        gbuf[spot * share : (spot + 1) * share] = gacc[chunk * share : (chunk + 1) * share].astype(BF16)
    vec[0] = jnp.concatenate([jnp.sum(vacc[k], axis=0, keepdims=True) for k in range(2)], axis=0)
    small = [
        mesh_lane(),
        grid_lane(gbuf, gbuf_in, dgrid_ref, wrecv_ref, grid_sem, n_level),
        vec_lane(vec, vec_in, dvec_ref, vec_sem, steps),
    ]
    advance(small)
    lanes = lanes + small + out_lanes
    while lanes:
        advance(lanes)


def body(
    grid_latent,
    mesh_latent,
    grid_output_cotangent,
    w_send,
    w_recv,
    output_weight,
    hidden_layer_bias,
    output_norm_gain,
    edge_sender,
    edge_receiver,
    edge_live,
):
    n_space = lax.axis_size("space")
    n_level = lax.axis_size("level")
    rows, width = grid_latent.shape
    mrows = mesh_latent.shape[1]
    slots = edge_sender.shape[1]
    block = min(256, slots)
    pad = -(-3 * mrows // 128) * 128
    mpad = -(-3 * mrows // TILE) * TILE
    steps = bit_steps("level", n_level) + bit_steps("space", n_space)
    n = len(steps)
    inbox = inbox_rows(width, steps)
    vm = pl.BlockSpec(memory_space=pltpu.VMEM)
    dma = pltpu.SemaphoreType.DMA
    everyone = n_space * n_level
    d_grid, d_mesh, d_w_out, d_w_recv, d_w_send, d_vec = pl.pallas_call(
        functools.partial(kernel, n_space, n_level, block, min(4, slots // block)),
        out_shape=(
            jax.ShapeDtypeStruct((rows // n_level, width), F32),
            jax.ShapeDtypeStruct((mrows, width), F32),
            jax.ShapeDtypeStruct((width, width), BF16),
            jax.ShapeDtypeStruct((width, width), BF16),
            jax.ShapeDtypeStruct((width, width), BF16),
            jax.ShapeDtypeStruct((2, width), F32),
        ),
        in_specs=[vm] * 11,
        out_specs=(vm,) * 6,
        scratch_shapes=[
            pltpu.VMEM((3, mrows, width), BF16),
            pltpu.VMEM((pad, width), BF16),
            pltpu.VMEM((rows, width), BF16),
            pltpu.VMEM((slots, width), F32),
            pltpu.VMEM((slots, width), BF16),
            pltpu.VMEM((slots, width), BF16),
            pltpu.VMEM((width, width), F32),
            pltpu.VMEM((rows, width), F32),
            pltpu.VMEM((mpad, width), F32),
            pltpu.VMEM((2, 8, width), F32),
            pltpu.VMEM((width, width), BF16),
            pltpu.VMEM((width, width), BF16),
            pltpu.VMEM((4, inbox, width // 2), BF16),
            pltpu.VMEM((rows, width), BF16),
            pltpu.VMEM((rows, width), BF16),
            pltpu.VMEM((n + 1, 2, width), F32),
            pltpu.VMEM((n, 2, width), F32),
            pltpu.VMEM((2, mrows, width), F32),
            pltpu.VMEM((2, mrows, width), F32),
            pltpu.VMEM((everyone, mrows, width), BF16),
            pltpu.VMEM((everyone, mrows, width), BF16),
            dma((2, 2)),
            dma((2, 2)),
            dma((4, n, 2)),
            dma((4, n, 2)),
            dma((2, n, 2)),
            dma((n, 2)),
            dma((n, 2)),
        ],
        compiler_params=pltpu.CompilerParams(collective_id=0, has_side_effects=True),
        name="edge_backward",
    )(
        grid_latent,
        mesh_latent[0],
        grid_output_cotangent,
        w_send,
        w_recv,
        output_weight,
        hidden_layer_bias[None],
        output_norm_gain[None],
        edge_sender,
        edge_receiver,
        edge_live,
    )
    return (
        d_grid,
        d_mesh[None],
        d_w_send,
        d_w_recv,
        d_w_out,
        d_vec[0],
        d_vec[1],
    )


def solution(mesh):
    return jax.shard_map(
        body,
        mesh=mesh,
        in_specs=(
            P("space", None),
            P("level", "space", None),
            P("space", None),
            P(),
            P(),
            P(),
            P(),
            P(),
            P("level", "space"),
            P("level", "space"),
            P("level", "space"),
        ),
        out_specs=(P(("space", "level"), None), P("level", "space", None), P(), P(), P(), P(), P()),
        check_vma=False,
    )
```

time: 82.8 us -> 71.7 us (0.87)
  Pallas kernels: 76.7 us -> 63.9 us
  local copies, waits for them, and re-layouts: 5.22 us -> 6.9 us
    pallas_call x1, Pallas kernels: 76.7 us -> 63.9 us  [body(): pl.pallas_call(functools.partial(kernel, n_space, n_level, block, min(4,...]
    unnamed x6 -> x13, local copies, waits for them, and re-layouts: 1.32 us -> 5.55 us
    slice x1 -> x0, local copies, waits for them, and re-layouts: 2.57 us -> none  [body(): d_w[:width]]
where the time goes in v2:
time: 71.7 us; the launch traced here: 71.4 us
  Pallas kernels  63.9 us (89%)
  local copies, waits for them, and re-layouts  6.9 us (10%)
    pallas_call x1, Pallas kernels, body(): pl.pallas_call(functools.partial(kernel, n_space, n_level, block, min(4,...  63.9 us
    unnamed x13, local copies, waits for them, and re-layouts  5.55 us

profile of v2, /device:TPU:0, one launch (start us, length us, event | category | flops | bytes accessed | tf_op | source)
XLA Modules:
  0.0 71.4 jit_solution(11599140331541085714)
XLA Ops:
  0.6 63.9 %edge_backward.1 = (f32[128,512]{1,0:T(8,128)}, f32[8,512]{1,0:T(8,128)}, bf16[512,512]{1,0:T(8,128)(2,1)}, bf16[512,512]{1,0:T(8,128)(2,1)}, bf16[512,512]{1,0:T(8,128)(2,1)}, /*index=5*/f32[2,512]{1,0:T(2,128)}) custom-call(bf16[512,512]{1,0:T(8,128)(2,1)} %grid_ref.1, bf16[8,512]{1,0:T(8,128)(2,1)} %bitcast.7, bf16[512,512]{1,0:T(8,128)(2,1)} %cot_ref.1, ...), custom_call_target="tpu_custom_call" | custom-call | tf_op jit(solution)/shard_map/edge_backward/pallas_call | solution.py:455
  64.5 0.0 copy-start.2
  64.5 1.3 %fusion = (f32[1,512]{1,0:T(1,128)}, f32[1,512]{1,0:T(1,128)}) fusion(f32[2,512]{1,0:T(2,128)} %get-tuple-element.18), kind=kLoop, calls=%fused_computation | loop fusion | bytes 8192 | tf_op jit(solution)/shard_map/slice | solution.py:519
  65.9 0.0 copy-start.3
  65.9 1.7 %copy.23 = f32[128,512]{1,0:T(8,128)} copy(f32[128,512]{1,0:T(8,128)} %get-tuple-element.28) | data formatting | bytes 524288
  67.5 0.0 copy-done.3
  67.5 0.6 copy.24
  68.1 0.0 copy-done.2
  68.2 0.0 copy-start.1
  68.2 0.8 %copy.25 = bf16[512,512]{1,0:T(8,128)(2,1)} copy(bf16[512,512]{1,0:T(8,128)(2,1)S(1)} %copy-done.2) | data formatting | bytes 1048576
  68.9 0.4 copy-done.1
  69.4 0.0 copy-start
  69.4 0.8 %copy.26 = bf16[512,512]{1,0:T(8,128)(2,1)} copy(bf16[512,512]{1,0:T(8,128)(2,1)S(1)} %copy-done.1) | data formatting | bytes 1048576
  70.2 0.4 copy-done
  70.6 0.8 %copy.27 = bf16[512,512]{1,0:T(8,128)(2,1)} copy(bf16[512,512]{1,0:T(8,128)(2,1)S(1)} %copy-done) | data formatting | bytes 1048576
Async XLA Ops:
  64.5 3.7 %copy-start.2 = (bf16[512,512]{1,0:T(8,128)(2,1)S(1)}, bf16[512,512]{1,0:T(8,128)(2,1)}, u32[]{:S(2)}) copy-start(bf16[512,512]{1,0:T(8,128)(2,1)} %get-tuple-element.30) | copy-start | bytes 1572868
  65.9 1.7 %copy-start.3 = (f32[8,512]{1,0:T(8,128)S(1)}, f32[8,512]{1,0:T(8,128)}, u32[]{:S(2)}) copy-start(f32[8,512]{1,0:T(8,128)} %get-tuple-element.14) | copy-start | bytes 49156
  68.2 1.2 %copy-start.1 = (bf16[512,512]{1,0:T(8,128)(2,1)S(1)}, bf16[512,512]{1,0:T(8,128)(2,1)}, u32[]{:S(2)}) copy-start(bf16[512,512]{1,0:T(8,128)(2,1)} %get-tuple-element.31) | copy-start | bytes 1572868
  69.4 1.2 %copy-start = (bf16[512,512]{1,0:T(8,128)(2,1)S(1)}, bf16[512,512]{1,0:T(8,128)(2,1)}, u32[]{:S(2)}) copy-start(bf16[512,512]{1,0:T(8,128)(2,1)} %get-tuple-element.32) | copy-start | bytes 1572868

commit v3 on v2

--- a/solution.py
+++ b/solution.py
@@ -26,10 +26,24 @@
     return steps
 
 
-def partner(axis, width):
-    me = lax.axis_index(axis)
-    bit = (me // width) % 2
-    return bit, {axis: me + (1 - 2 * bit) * width}
+def exchange_groups(n_space, n_level):
+    bits = bit_steps("level", n_level) + bit_steps("space", n_space)
+    return [bits[:1]] + [bits[k : k + 2] for k in range(1, len(bits), 2)]
+
+
+def members(group):
+    bits = [(lax.axis_index(axis) // w) % 2 for axis, w in group]
+    mine = sum(bit << j for j, bit in enumerate(bits))
+    others = []
+    for mask in range(1, 1 << len(group)):
+        place, who = 0, {}
+        for j, (axis, w) in enumerate(group):
+            flip = (mask >> j) & 1
+            place = place + ((1 - bits[j]) if flip else bits[j]) * (1 << j)
+            if flip:
+                who[axis] = who.get(axis, lax.axis_index(axis)) + (1 - 2 * bits[j]) * w
+        others.append((place, who))
+    return mine, others
 
 
 def reversed_chunks(count):
@@ -41,25 +55,19 @@
     return order
 
 
-def step_orders(n_space, n_level):
-    level = bit_steps("level", n_level)
-    space = bit_steps("space", n_space)
-    return level + space, level[:-1] + space[:1] + level[-1:] + space[1:]
-
-
-def halvings(rows, steps):
+def pieces(rows, groups):
     plan = []
     size = rows
-    for axis, width in steps:
-        split = (size // 2) % TILE == 0
-        plan.append((axis, width, size, split))
-        if split:
-            size //= 2
+    for group in groups:
+        m = 1 << len(group)
+        split = (size // m) % TILE == 0
+        size = size // m if split else size
+        plan.append((group, size, split))
     return plan
 
 
-def inbox_rows(rows, steps):
-    return sum(size // 2 if split else size for _, _, size, split in halvings(rows, steps))
+def inbox_rows(rows, groups):
+    return sum(((1 << len(group)) - 1) * size for group, size, _ in pieces(rows, groups))
 
 
 def remote(src, dst, sem, who):
@@ -73,54 +81,71 @@
     )
 
 
-def reduce_lane(buf, out, inbox, cols, sem_r, sem_g, steps):
+def start_all(copies):
+    for c in copies:
+        c.start()
+
+
+def wait_all(copies):
+    for c in copies:
+        c.wait()
+
+
+def reduce_lane(buf, out, inbox, sem_r, sem_g, groups):
     off = 0
     spot = 0
     trail = []
-    for k, (axis, w, size, split) in enumerate(halvings(buf.shape[0], steps)):
-        bit, who = partner(axis, w)
-        half = size // 2 if split else size
-        give = off + (1 - bit) * half if split else off
-        keep = off + bit * half if split else off
-        at_give = pl.ds(pl.multiple_of(give, TILE), half)
-        at_keep = pl.ds(pl.multiple_of(keep, TILE), half)
-        into = pl.ds(spot, half)
-        c = remote(buf.at[at_give, cols], inbox.at[into], sem_r.at[k], who)
-        c.start()
-        yield
-        c.wait()
-        buf[at_keep, cols] = (buf[at_keep, cols].astype(F32) + inbox[into].astype(F32)).astype(BF16)
-        spot += half
-        off = keep
+    for k, (group, size, split) in enumerate(pieces(buf.shape[0], groups)):
+        mine, others = members(group)
+        copies, slots = [], []
+        for j, (place, who) in enumerate(others):
+            give = pl.ds(pl.multiple_of(off + place * size if split else off, TILE), size)
+            slot = pl.ds(spot, size)
+            copies.append(remote(buf.at[give], inbox.at[slot], sem_r.at[k, j], who))
+            slots.append(slot)
+            spot += size
+        start_all(copies)
+        yield
+        wait_all(copies)
+        off = off + mine * size if split else off
+        keep = pl.ds(pl.multiple_of(off, TILE), size)
+        total = buf[keep].astype(F32)
+        for slot in slots:
+            total = total + inbox[slot].astype(F32)
+        buf[keep] = total.astype(BF16)
         if split:
-            trail.append((k, who, half, bit))
-    at = pl.ds(pl.multiple_of(off, TILE), trail[-1][2])
-    out[at, cols] = buf[at, cols]
-    for k, who, half, bit in reversed(trail):
-        at = pl.ds(pl.multiple_of(off, TILE), half)
-        c = remote(out.at[at, cols], out.at[at, cols], sem_g.at[k], who)
-        c.start()
-        yield
-        c.wait()
-        off = off - bit * half
-
-
-def gather_lane(buf, sem, steps):
-    base = gather_place(steps)
-    for j, (axis, w) in enumerate(reversed(steps)):
-        bit, who = partner(axis, w)
-        at = pl.ds(base, 1 << j)
-        c = remote(buf.at[at], buf.at[at], sem.at[j], who)
-        c.start()
-        yield
-        c.wait()
-        base = base - bit * (1 << j)
-
-
-def gather_place(steps):
+            trail.append((k, mine, others, size))
+    at = pl.ds(pl.multiple_of(off, TILE), trail[-1][3])
+    out[at] = buf[at]
+    for k, mine, others, size in reversed(trail):
+        at = pl.ds(pl.multiple_of(off, TILE), size)
+        copies = [remote(out.at[at], out.at[at], sem_g.at[k, j], who) for j, (_, who) in enumerate(others)]
+        start_all(copies)
+        yield
+        wait_all(copies)
+        off = off - mine * size
+
+
+def gather_lane(buf, sem, groups):
+    base = gather_place(groups)
+    held = 1
+    for k, group in enumerate(reversed(groups)):
+        mine, others = members(group)
+        at = pl.ds(base, held)
+        copies = [remote(buf.at[at], buf.at[at], sem.at[k, j], who) for j, (_, who) in enumerate(others)]
+        start_all(copies)
+        yield
+        wait_all(copies)
+        base = base - mine * held
+        held <<= len(group)
+
+
+def gather_place(groups):
     place = 0
-    for j, (axis, w) in enumerate(reversed(steps)):
-        place = place + partner(axis, w)[0] * (1 << j)
+    held = 1
+    for group in reversed(groups):
+        place = place + members(group)[0] * held
+        held <<= len(group)
     return place
 
 
@@ -129,7 +154,7 @@
     size = gbuf.shape[0]
     spot = 0
     for k, (axis, w) in enumerate(bit_steps("level", n_level)):
-        bit, who = partner(axis, w)
+        bit, [(_, who)] = members([(axis, w)])
         size //= 2
         give = pl.ds(pl.multiple_of(off + (1 - bit) * size, TILE), size)
         keep = pl.ds(pl.multiple_of(off + bit * size, TILE), size)
@@ -144,15 +169,20 @@
     dgrid_ref[...] = mm(gbuf[pl.ds(pl.multiple_of(off, TILE), size)], wrecv_ref[...], 1, 1)
 
 
-def vec_lane(vec, inbox, dvec_ref, sem, steps):
-    for k, (axis, w) in enumerate(steps):
-        _, who = partner(axis, w)
-        c = remote(vec.at[k], inbox.at[k], sem.at[k], who)
-        c.start()
-        yield
-        c.wait()
-        vec[k + 1] = vec[k] + inbox[k]
-    dvec_ref[...] = vec[len(steps)]
+def vec_lane(vec, inbox, dvec_ref, sem, groups):
+    for k, group in enumerate(groups):
+        _, others = members(group)
+        copies = [
+            remote(vec.at[k], inbox.at[k, j], sem.at[k, j], who) for j, (_, who) in enumerate(others)
+        ]
+        start_all(copies)
+        yield
+        wait_all(copies)
+        if len(others) == 3:
+            vec[k + 1] = (vec[k] + inbox[k, 0]) + (inbox[k, 1] + inbox[k, 2])
+        else:
+            vec[k + 1] = vec[k] + inbox[k, 0]
+    dvec_ref[...] = vec[len(groups)]
 
 
 def edge_copies(up, down):
@@ -245,14 +275,14 @@
     mrows = mesh_ref.shape[0]
     slots = snd_ref.shape[1]
     band = lax.axis_index("space")
-    steps, swapped = step_orders(n_space, n_level)
+    groups = exchange_groups(n_space, n_level)
     pad = table.shape[0]
 
     window[...] = jnp.zeros_like(window)
     m_in[...] = jnp.zeros_like(m_in)
     barrier = pltpu.get_barrier_semaphore()
-    for axis, w in steps:
-        _, who = partner(axis, w)
+    peers = [who for group in groups for _, who in members(group)[1]]
+    for who in peers:
         pl.semaphore_signal(barrier, inc=1, device_id=who, device_id_type=MESH)
     up = {"space": (band + 1) % n_space}
     down = {"space": (band + n_space - 1) % n_space}
@@ -263,17 +293,17 @@
     gacc[...] = jnp.zeros_like(gacc)
     vacc[...] = jnp.zeros_like(vacc)
     window[1] = mesh_ref[...]
-    place = gather_place(steps)
+    place = gather_place(groups)
     mesh_all[place] = mesh_ref[...]
     proj[...] = mm(grid_ref[...], wrecv_ref[...]).astype(BF16)
-    pl.semaphore_wait(barrier, len(steps) + 2)
+    pl.semaphore_wait(barrier, len(peers) + 2)
 
     halo_start, halo_wait = edge_copies(
         remote(mesh_ref, window.at[0], halo_sem.at[0], up),
         remote(mesh_ref, window.at[2], halo_sem.at[1], down),
     )
     halo_start()
-    early = [gather_lane(mesh_all, mesh_sem.at[0], steps)]
+    early = [gather_lane(mesh_all, mesh_sem.at[0], groups)]
     advance(early)
 
     def span(i):
@@ -363,17 +393,11 @@
         lax.fori_loop(lo, hi, forward, 0)
         advance(early)
 
-    half = width // 2
-    sides = [(pl.ds(0, half), steps), (pl.ds(half, half), swapped)]
-
-    def reducers(buf, out, at):
-        return [
-            reduce_lane(buf, out, inbox.at[at + k], cols, red_sem.at[at + k], gat_sem.at[at + k], order)
-            for k, (cols, order) in enumerate(sides)
-        ]
+    def reducer(buf, out, k):
+        return reduce_lane(buf, out, inbox.at[k], red_sem.at[k], gat_sem.at[k], groups)
 
     red_o[...] = wacc[...].astype(BF16)
-    out_lanes = reducers(red_o, dwo_ref, 0) + early
+    out_lanes = [reducer(red_o, dwo_ref, 0)] + early
     advance(out_lanes)
     for lo, hi in zip(cuts, cuts[1:]):
         lax.fori_loop(lo, hi, backward, 0)
@@ -381,7 +405,7 @@
             advance(out_lanes)
 
     red_r[...] = mm(grid_ref[...], gacc[...].astype(BF16), 0, 0).astype(BF16)
-    lanes = reducers(red_r, dwr_ref, 2)
+    lanes = [reducer(red_r, dwr_ref, 1)]
     advance(lanes)
 
     def mesh_lane():
@@ -396,7 +420,7 @@
         wait()
         total = macc[mrows : 2 * mrows] + m_in[0] + m_in[1]
         sum_all[place] = total.astype(BF16)
-        lane = gather_lane(sum_all, mesh_sem.at[1], steps)
+        lane = gather_lane(sum_all, mesh_sem.at[1], groups)
         next(lane)
         total = jnp.concatenate([total, jnp.zeros((TILE - mrows % TILE, width), F32)], axis=0)
         dmesh_ref[...] = mm(total.astype(BF16), wsend_ref[...], 1, 1)[0:mrows]
@@ -417,7 +441,7 @@
     small = [
         mesh_lane(),
         grid_lane(gbuf, gbuf_in, dgrid_ref, wrecv_ref, grid_sem, n_level),
-        vec_lane(vec, vec_in, dvec_ref, vec_sem, steps),
+        vec_lane(vec, vec_in, dvec_ref, vec_sem, groups),
     ]
     advance(small)
     lanes = lanes + small + out_lanes
@@ -446,9 +470,9 @@
     block = min(256, slots)
     pad = -(-3 * mrows // 128) * 128
     mpad = -(-3 * mrows // TILE) * TILE
-    steps = bit_steps("level", n_level) + bit_steps("space", n_space)
-    n = len(steps)
-    inbox = inbox_rows(width, steps)
+    groups = exchange_groups(n_space, n_level)
+    n = len(groups)
+    inbox = inbox_rows(width, groups)
     vm = pl.BlockSpec(memory_space=pltpu.VMEM)
     dma = pltpu.SemaphoreType.DMA
     everyone = n_space * n_level
@@ -477,22 +501,22 @@
             pltpu.VMEM((2, 8, width), F32),
             pltpu.VMEM((width, width), BF16),
             pltpu.VMEM((width, width), BF16),
-            pltpu.VMEM((4, inbox, width // 2), BF16),
+            pltpu.VMEM((2, inbox, width), BF16),
             pltpu.VMEM((rows, width), BF16),
             pltpu.VMEM((rows, width), BF16),
             pltpu.VMEM((n + 1, 2, width), F32),
-            pltpu.VMEM((n, 2, width), F32),
+            pltpu.VMEM((n, 3, 2, width), F32),
             pltpu.VMEM((2, mrows, width), F32),
             pltpu.VMEM((2, mrows, width), F32),
             pltpu.VMEM((everyone, mrows, width), BF16),
             pltpu.VMEM((everyone, mrows, width), BF16),
             dma((2, 2)),
             dma((2, 2)),
-            dma((4, n, 2)),
-            dma((4, n, 2)),
-            dma((2, n, 2)),
-            dma((n, 2)),
-            dma((n, 2)),
+            dma((2, n, 3, 2)),
+            dma((2, n, 3, 2)),
+            dma((2, n, 3, 2)),
+            dma((len(bit_steps("level", n_level)), 2)),
+            dma((n, 3, 2)),
         ],
         compiler_params=pltpu.CompilerParams(collective_id=0, has_side_effects=True),
         name="edge_backward",

time: 71.7 us -> 67.9 us (0.947)
  Pallas kernels: 63.9 us -> 60 us
    pallas_call x1, Pallas kernels: 63.9 us -> 60 us  [body(): pl.pallas_call(functools.partial(kernel, n_space, n_level, block, min(4,...]
where the time goes in v3:
time: 67.9 us; the launch traced here: 67.6 us
  Pallas kernels  60 us (88%)
  local copies, waits for them, and re-layouts  6.9 us (10%)
    pallas_call x1, Pallas kernels, body(): pl.pallas_call(functools.partial(kernel, n_space, n_level, block, min(4,...  60 us
    unnamed x13, local copies, waits for them, and re-layouts  5.55 us

profile of v3, /device:TPU:0, one launch (start us, length us, event | category | flops | bytes accessed | tf_op | source)
XLA Modules:
  0.0 67.6 jit_solution(6527975287382098756)
XLA Ops:
  0.6 60.0 %edge_backward.1 = (f32[128,512]{1,0:T(8,128)}, f32[8,512]{1,0:T(8,128)}, bf16[512,512]{1,0:T(8,128)(2,1)}, bf16[512,512]{1,0:T(8,128)(2,1)}, bf16[512,512]{1,0:T(8,128)(2,1)}, /*index=5*/f32[2,512]{1,0:T(2,128)}) custom-call(bf16[512,512]{1,0:T(8,128)(2,1)} %grid_ref.1, bf16[8,512]{1,0:T(8,128)(2,1)} %bitcast.7, bf16[512,512]{1,0:T(8,128)(2,1)} %cot_ref.1, ...), custom_call_target="tpu_custom_call" | custom-call | tf_op jit(solution)/shard_map/edge_backward/pallas_call | solution.py:479
  60.6 0.0 copy-start.2
  60.7 1.3 %fusion = (f32[1,512]{1,0:T(1,128)}, f32[1,512]{1,0:T(1,128)}) fusion(f32[2,512]{1,0:T(2,128)} %get-tuple-element.18), kind=kLoop, calls=%fused_computation | loop fusion | bytes 8192 | tf_op jit(solution)/shard_map/slice | solution.py:543
  62.0 0.0 copy-start.3
  62.0 1.7 %copy.23 = f32[128,512]{1,0:T(8,128)} copy(f32[128,512]{1,0:T(8,128)} %get-tuple-element.28) | data formatting | bytes 524288
  63.7 0.0 copy-done.3
  63.7 0.6 copy.24
  64.3 0.0 copy-done.2
  64.3 0.0 copy-start.1
  64.3 0.8 %copy.25 = bf16[512,512]{1,0:T(8,128)(2,1)} copy(bf16[512,512]{1,0:T(8,128)(2,1)S(1)} %copy-done.2) | data formatting | bytes 1048576
  65.1 0.4 copy-done.1
  65.5 0.0 copy-start
  65.5 0.8 %copy.26 = bf16[512,512]{1,0:T(8,128)(2,1)} copy(bf16[512,512]{1,0:T(8,128)(2,1)S(1)} %copy-done.1) | data formatting | bytes 1048576
  66.3 0.4 copy-done
  66.8 0.8 %copy.27 = bf16[512,512]{1,0:T(8,128)(2,1)} copy(bf16[512,512]{1,0:T(8,128)(2,1)S(1)} %copy-done) | data formatting | bytes 1048576
Async XLA Ops:
  60.6 3.7 %copy-start.2 = (bf16[512,512]{1,0:T(8,128)(2,1)S(1)}, bf16[512,512]{1,0:T(8,128)(2,1)}, u32[]{:S(2)}) copy-start(bf16[512,512]{1,0:T(8,128)(2,1)} %get-tuple-element.30) | copy-start | bytes 1572868
  62.0 1.7 %copy-start.3 = (f32[8,512]{1,0:T(8,128)S(1)}, f32[8,512]{1,0:T(8,128)}, u32[]{:S(2)}) copy-start(f32[8,512]{1,0:T(8,128)} %get-tuple-element.14) | copy-start | bytes 49156
  64.3 1.2 %copy-start.1 = (bf16[512,512]{1,0:T(8,128)(2,1)S(1)}, bf16[512,512]{1,0:T(8,128)(2,1)}, u32[]{:S(2)}) copy-start(bf16[512,512]{1,0:T(8,128)(2,1)} %get-tuple-element.31) | copy-start | bytes 1572868
  65.5 1.2 %copy-start = (bf16[512,512]{1,0:T(8,128)(2,1)S(1)}, bf16[512,512]{1,0:T(8,128)(2,1)}, u32[]{:S(2)}) copy-start(bf16[512,512]{1,0:T(8,128)(2,1)} %get-tuple-element.32) | copy-start | bytes 1572868

commit v4 on v3

--- a/solution.py
+++ b/solution.py
@@ -449,6 +449,45 @@
         advance(lanes)
 
 
+def hand_out(
+    grid_in,
+    mesh_in,
+    wo_in,
+    wr_in,
+    ws_in,
+    vec_in,
+    grid_out,
+    mesh_out,
+    wo_out,
+    wr_out,
+    ws_out,
+    bias_out,
+    gain_out,
+    grid_mid,
+    mesh_mid,
+    wo_mid,
+    wr_mid,
+    ws_mid,
+    sem,
+):
+    trips = [
+        (grid_in, grid_mid, grid_out),
+        (mesh_in, mesh_mid, mesh_out.at[0]),
+        (wo_in, wo_mid, wo_out),
+        (wr_in, wr_mid, wr_out),
+        (ws_in, ws_mid, ws_out),
+    ]
+    loads = [pltpu.make_async_copy(a, b, sem.at[0, k]) for k, (a, b, _) in enumerate(trips)]
+    stores = [pltpu.make_async_copy(b, c, sem.at[1, k]) for k, (_, b, c) in enumerate(trips)]
+    start_all(loads)
+    bias_out[...] = vec_in[0]
+    gain_out[...] = vec_in[1]
+    for load, store in zip(loads, stores):
+        load.wait()
+        store.start()
+    wait_all(stores)
+
+
 def body(
     grid_latent,
     mesh_latent,
@@ -467,7 +506,7 @@
     rows, width = grid_latent.shape
     mrows = mesh_latent.shape[1]
     slots = edge_sender.shape[1]
-    block = min(256, slots)
+    block = min(512, slots)
     pad = -(-3 * mrows // 128) * 128
     mpad = -(-3 * mrows // TILE) * TILE
     groups = exchange_groups(n_space, n_level)
@@ -533,15 +572,31 @@
         edge_receiver,
         edge_live,
     )
-    return (
-        d_grid,
-        d_mesh[None],
-        d_w_send,
-        d_w_recv,
-        d_w_out,
-        d_vec[0],
-        d_vec[1],
-    )
+    hbm = pl.BlockSpec(memory_space=pl.ANY)
+    d_grid, d_mesh, d_w_out, d_w_recv, d_w_send, d_bias, d_gain = pl.pallas_call(
+        hand_out,
+        out_shape=(
+            jax.ShapeDtypeStruct(d_grid.shape, F32),
+            jax.ShapeDtypeStruct((1,) + d_mesh.shape, F32),
+            jax.ShapeDtypeStruct(d_w_out.shape, BF16),
+            jax.ShapeDtypeStruct(d_w_recv.shape, BF16),
+            jax.ShapeDtypeStruct(d_w_send.shape, BF16),
+            jax.ShapeDtypeStruct((width,), F32),
+            jax.ShapeDtypeStruct((width,), F32),
+        ),
+        in_specs=[hbm] * 5 + [vm],
+        out_specs=(hbm,) * 5 + (vm,) * 2,
+        scratch_shapes=[
+            pltpu.VMEM(d_grid.shape, F32),
+            pltpu.VMEM(d_mesh.shape, F32),
+            pltpu.VMEM(d_w_out.shape, BF16),
+            pltpu.VMEM(d_w_recv.shape, BF16),
+            pltpu.VMEM(d_w_send.shape, BF16),
+            dma((2, 5)),
+        ],
+        name="hand_out",
+    )(d_grid, d_mesh, d_w_out, d_w_recv, d_w_send, d_vec)
+    return (d_grid, d_mesh, d_w_send, d_w_recv, d_w_out, d_bias, d_gain)
 
 
 def solution(mesh):

time: 67.9 us -> 61.2 us (0.901)
  local copies, waits for them, and re-layouts: 6.9 us -> 0 us
    unnamed x13 -> x0, local copies, waits for them, and re-layouts: 5.55 us -> none
    pallas_call x0 -> x1, Pallas kernels: none -> 3.62 us  [body(): pl.pallas_call(hand_out, out_shape=(jax.ShapeDtypeStruct(d_grid.shape, F3...]
    pallas_call x1, Pallas kernels: 60 us -> 56.7 us  [body(): pl.pallas_call(functools.partial(kernel, n_space, n_level, block, min(4,...]
    slice x1 -> x0, local copies, waits for them, and re-layouts: 1.35 us -> none  [body(): d_vec[1]]
where the time goes in v4:
time: 61.2 us; the launch traced here: 61 us
  Pallas kernels  60.4 us (99%)
  between operations  0.64 us (1%)
    pallas_call x1, Pallas kernels, body(): pl.pallas_call(functools.partial(kernel, n_space, n_level, block, min(4,...  56.7 us
    pallas_call x1, Pallas kernels, body(): pl.pallas_call(hand_out, out_shape=(jax.ShapeDtypeStruct(d_grid.shape, F3...  3.62 us

profile of v4, /device:TPU:0, one launch (start us, length us, event | category | flops | bytes accessed | tf_op | source)
XLA Modules:
  0.0 61.0 jit_solution(3628875611637575686)
XLA Ops:
  0.6 56.7 %edge_backward.1 = (f32[128,512]{1,0:T(8,128)}, f32[8,512]{1,0:T(8,128)}, bf16[512,512]{1,0:T(8,128)(2,1)}, bf16[512,512]{1,0:T(8,128)(2,1)}, bf16[512,512]{1,0:T(8,128)(2,1)}, /*index=5*/f32[2,512]{1,0:T(2,128)}) custom-call(bf16[512,512]{1,0:T(8,128)(2,1)} %grid_ref.1, bf16[8,512]{1,0:T(8,128)(2,1)} %bitcast.3, bf16[512,512]{1,0:T(8,128)(2,1)} %cot_ref.1, ...), custom_call_target="tpu_custom_call" | custom-call | tf_op jit(solution)/shard_map/edge_backward/pallas_call | solution.py:518
  57.4 3.6 %hand_out.1 = (f32[128,512]{1,0:T(8,128)}, f32[1,8,512]{2,1,0:T(8,128)}, bf16[512,512]{1,0:T(8,128)(2,1)}, bf16[512,512]{1,0:T(8,128)(2,1)}, bf16[512,512]{1,0:T(8,128)(2,1)}, /*index=5*/f32[512]{0:T(512)}, f32[512]{0:T(512)}) custom-call(f32[128,512]{1,0:T(8,128)} %get-tuple-element.20.grid_in, f32[8,512]{1,0:T(8,128)} %get-tuple-element.21.mesh_in, ...), custom_call_target="tpu_custom_call" | custom-call | tf_op jit(solution)/shard_map/hand_out/pallas_call | solution.py:576
